TPU v7x, 32 devices: a whole 2x2x4 slice. The times are simulated.
32 devices in a mesh: seq: 2 (over core), width: 4 (over y, x), dp: 4 (over z).
Axes of the slice: x: 2, y: 2, z: 4, core: 2. Of those that a mesh axis runs over, the one named last changes fastest.
Arguments:
- inputs: bfloat16 [4, 512, 5376], P('dp', 'seq', 'width'), may hold values from -6 to 6
- out_grad: bfloat16 [4, 512, 5376], P('dp', 'seq', 'width'), may hold values from -6 to 6
- gate_a: bfloat16 [16, 336, 336], P('width'), may hold values from -0.3125 to 0.3125
- gate_x: bfloat16 [16, 336, 336], P('width'), may hold values from -0.3125 to 0.3125
- bias_a: float32 [5376], P('width'), may hold values from -1.5 to 1.5
- bias_x: float32 [5376], P('width'), may hold values from -1.5 to 1.5
- decay_param: float32 [5376], P('width'), may hold values from -12 to -4.5
- segment_ids: int32 [4, 512], P('dp', 'seq'), may hold values from 0 to 3, never falling along the last dimension, each value on 1 to 256 neighbouring positions
Outputs:
- input_grad: bfloat16 [4, 512, 5376], P('dp', 'seq', 'width')
- gate_a_grad: float32 [16, 336, 336], P('width')
- gate_x_grad: float32 [16, 336, 336], P('width')
- bias_a_grad: float32 [5376], P('width')
- bias_x_grad: float32 [5376], P('width')
- decay_grad: float32 [5376], P('width')
All inputs are finite; a program needn't handle non-finite values.
Results may differ from a plain program's by a relative error of at most 0.0029.
Values sent between devices are 32-bit elements; how exact they have to be, the bound alone decides.
No kernel may reach another device: no remote copies, remote signals or barrier semaphores. Data moves between devices by JAX's collectives and lax.ppermute only.
A program may use at most 128 MiB of HBM per device.

v0:
```python
import jax
import jax.numpy as jnp
from jax import lax
from jax.sharding import PartitionSpec as P


def shifted(value, axis, steps):
    count = lax.axis_size(axis)
    initial, last = (max(0, -steps), min(count, count - steps))
    return lax.ppermute(value, axis, [(source, source + steps) for source in range(initial, last)])


def carried_in(value, axis, join, neutral, backward):
    count, mine = (lax.axis_size(axis), lax.axis_index(axis))
    pieces = jax.tree.map(lambda part: lax.all_gather(part, axis), value)
    if backward:
        pieces = jax.tree.map(lambda part: part[::-1], pieces)
        mine = count - 1 - mine
    running = jax.tree.map(
        lambda part, zero: jnp.full_like(part, 0) + jnp.asarray(zero, part.dtype), value, neutral
    )

    def hop(position, running):
        longer = join(running, jax.tree.map(lambda part: part[position], pieces))
        return jax.tree.map(lambda new, old: jnp.where(position < mine, new, old), longer, running)

    return lax.fori_loop(0, count - 1, hop, running)


def combine(earlier, later):
    return (earlier[0] * later[0], earlier[1] * later[0] + later[1])


def shards(inputs, out_grad, gate_a, gate_x, bias_a, bias_x, decay_param, segment_ids):
    batch, count, chans = inputs.shape
    blocks, width_k = (gate_a.shape[0], gate_a.shape[1])
    span_len = 8
    groups = count // span_len
    blocked = inputs.reshape(batch, count, blocks, width_k)
    pre_a = (
        jnp.einsum("stbk,bkj->stbj", blocked, gate_a, preferred_element_type=jnp.float32).reshape(
            batch, count, chans
        )
        + bias_a
    )
    pre_x = (
        jnp.einsum("stbk,bkj->stbj", blocked, gate_x, preferred_element_type=jnp.float32).reshape(
            batch, count, chans
        )
        + bias_x
    )
    rate = jax.nn.sigmoid(pre_a)
    ingate = jax.nn.sigmoid(pre_x)
    soft = jax.nn.softplus(decay_param)
    log_a = -8.0 * rate * soft
    decay = jnp.exp(log_a)
    shifted_ids = segment_ids + 1
    before = shifted(shifted_ids[:, -1:], "seq", 1)
    previous = jnp.concatenate([before, shifted_ids[:, :-1]], 1)
    position = lax.axis_index("seq") * count + jnp.arange(count, dtype=jnp.int32)
    reset = (shifted_ids != previous) | (position[None, :] == 0)
    keep = jnp.where(reset, 0.0, 1.0).astype(jnp.float32)[:, :, None]
    abar = keep * decay
    mult = jnp.where(keep > 0.5, jnp.sqrt(-jnp.expm1(2.0 * log_a)), 1.0)
    xf = inputs.astype(jnp.float32)
    dyf = out_grad.astype(jnp.float32)
    drive = mult * ingate * xf
    cum_log = jnp.cumsum(log_a.reshape(batch, groups, span_len, chans), 2)
    cum_reset = jnp.cumsum(
        jnp.where(reset, 1.0, 0.0).astype(jnp.float32).reshape(batch, groups, span_len), 2
    )
    order = jnp.arange(span_len, dtype=jnp.int32)
    lower = order[:, None] >= order[None, :]
    linked = (cum_reset[:, :, :, None] == cum_reset[:, :, None, :]) & lower
    spread = cum_log[:, :, :, None, :] - cum_log[:, :, None, :, :]
    factor = jnp.where(linked[..., None], jnp.exp(jnp.minimum(spread, 0.0)), 0.0)
    state_loc = jnp.einsum(
        "bntsc,bnsc->bntc",
        factor,
        drive.reshape(batch, groups, span_len, chans),
        precision=lax.Precision.HIGHEST,
    )
    grad_loc = jnp.einsum(
        "bntsc,bntc->bnsc",
        factor,
        dyf.reshape(batch, groups, span_len, chans),
        precision=lax.Precision.HIGHEST,
    )
    from_start = jnp.exp(cum_log) * jnp.where(cum_reset == 0.0, 1.0, 0.0)[..., None]
    to_end = (
        jnp.exp(cum_log[:, :, -1:, :] - cum_log)
        * jnp.where(cum_reset == cum_reset[:, :, -1:], 1.0, 0.0)[..., None]
    )
    group_prod = from_start[:, :, -1]
    group_state = state_loc[:, :, -1]
    group_grad = abar.reshape(batch, groups, span_len, chans)[:, :, 0] * grad_loc[:, :, 0]
    fwd_p, fwd_s = lax.associative_scan(combine, (group_prod, group_state), axis=1)
    bwd_p, bwd_s = lax.associative_scan(combine, (group_prod, group_grad), reverse=True, axis=1)
    forward_sum = (fwd_p[:, -1], fwd_s[:, -1])
    backward_sum = (bwd_p[:, 0], bwd_s[:, 0])
    unit = jnp.ones((batch, chans), jnp.float32)
    naught = jnp.zeros((batch, chans), jnp.float32)
    state_in = carried_in(forward_sum, "seq", combine, (unit, naught), False)[1]
    grad_in = carried_in(backward_sum, "seq", combine, (unit, naught), True)[1]
    excl_p = jnp.concatenate([unit[:, None], fwd_p[:, :-1]], 1)
    excl_s = jnp.concatenate([naught[:, None], fwd_s[:, :-1]], 1)
    entering = excl_s + excl_p * state_in[:, None, :]
    later_p = jnp.concatenate([bwd_p[:, 1:], unit[:, None]], 1)
    later_s = jnp.concatenate([bwd_s[:, 1:], naught[:, None]], 1)
    leaving = later_s + later_p * grad_in[:, None, :]
    state = (state_loc + from_start * entering[:, :, None, :]).reshape(batch, count, chans)
    grad = (grad_loc + to_end * leaving[:, :, None, :]).reshape(batch, count, chans)
    wsum = grad * (state - drive) - keep * (grad * ingate * xf * decay * decay / mult)
    dpre_a = -8.0 * soft * rate * (1.0 - rate) * wsum
    dpre_x = grad * mult * xf * ingate * (1.0 - ingate)
    da_b = dpre_a.astype(jnp.bfloat16).reshape(batch, count, blocks, width_k)
    dx_b = dpre_x.astype(jnp.bfloat16).reshape(batch, count, blocks, width_k)
    back = jnp.einsum(
        "stbj,bkj->stbk", da_b, gate_a, preferred_element_type=jnp.float32
    ) + jnp.einsum("stbj,bkj->stbk", dx_b, gate_x, preferred_element_type=jnp.float32)
    input_grad = (grad * mult * ingate + back.reshape(batch, count, chans)).astype(jnp.bfloat16)
    local_a = jnp.einsum("stbk,stbj->bkj", blocked, da_b, preferred_element_type=jnp.float32)
    local_x = jnp.einsum("stbk,stbj->bkj", blocked, dx_b, preferred_element_type=jnp.float32)
    bias_ga = jnp.sum(dpre_a, (0, 1))
    bias_gx = jnp.sum(dpre_x, (0, 1))
    decay_g = jnp.sum(-8.0 * rate * wsum, (0, 1))
    grad_a, grad_x, bias_ga, bias_gx, decay_g = lax.psum(
        (local_a, local_x, bias_ga, bias_gx, decay_g), ("seq", "dp")
    )
    return (input_grad, grad_a, grad_x, bias_ga, bias_gx, jax.nn.sigmoid(decay_param) * decay_g)


def solution(mesh):
    in_specs = (
        P("dp", "seq", "width"),
        P("dp", "seq", "width"),
        P("width", None, None),
        P("width", None, None),
        P("width"),
        P("width"),
        P("width"),
        P("dp", "seq"),
    )
    out_specs = (
        P("dp", "seq", "width"),
        P("width", None, None),
        P("width", None, None),
        P("width"),
        P("width"),
        P("width"),
    )
    return jax.shard_map(shards, mesh=mesh, in_specs=in_specs, out_specs=out_specs, check_vma=False)
```

profile of v0, /device:TPU:0, one launch (start us, length us, event | category | flops | bytes accessed | tf_op | source)
XLA Modules:
  0.0 415.5 jit_solution(12818486162488649593)
XLA Ops:
  8.6 2.9 collective-permute-start
  12.2 2.3 copy.78
  19.0 2.9 copy.77
  25.0 2.1 reshape.984
  28.6 6.4 %reduce_window_sum.23 = f32[1,32,8,1344]{3,2,1,0:T(8,128)S(1)} reduce-window(f32[1,32,8,1344]{3,2,1,0:T(8,128)} %divide_multiply_fusion, f32[]{:T(128)} %constant.20.clone.1), window={size=1x1x8x1 pad=0_0x0_0x7_0x0_0}, to_apply=%region_1.2 | reduce-window | flops 2408448 | bytes 2752516 | tf_op jit(solution)/shard_map/jit(cumsum)/reduce_window_sum | solution.py:68
  37.2 4.8 %multiply_reduce_fusion.1 = f32[32,1344,8]{1,2,0:T(8,128)S(1)} fusion(f32[32,1344,8]{1,2,0:T(8,128)} %bitcast_convert_fusion, f32[32,8,1344]{2,1,0:T(8,128)S(1)} %bitcast.111, pred[32,8,8]{2,1,0:T(8,128)(4,1)S(1)} %compare_and_fusion), kind=kLoop, calls=%fused_computation.1 | loop fusion | flops 13418496 | bytes 4130816 | tf_op jit(solution)/shard_map/bntsc,bntc->bnsc/dot_general | solution.py:83
  47.9 15.7 %multiply_reduce_fusion = f32[32,1344,8]{1,2,0:T(8,128)S(1)} fusion(f32[32,1344,8]{1,2,0:T(8,128)S(1)} %fusion.6, f32[32,8,1344]{2,1,0:T(8,128)S(1)} %bitcast.112, pred[32,8,8]{2,1,0:T(8,128)(4,1)S(1)} %compare_and_fusion), kind=kLoop, calls=%fused_computation | loop fusion | flops 13418496 | bytes 4130816 | tf_op jit(solution)/shard_map/bntsc,bnsc->bntc/dot_general | solution.py:77
  87.1 3.2 pad.142
  91.6 3.2 pad.132
  94.8 3.2 pad.133
  98.0 3.2 pad.143
  113.1 1.9 pad.150
  116.9 1.9 pad.161
  120.2 1.9 pad.160
  127.6 3.2 pad.162
  132.2 3.2 pad.152
  135.4 3.2 pad.153
  138.6 3.2 pad.163
  147.7 4.7 %pad.164 = f32[1,16,1344]{2,0,1:T(1,128)} pad(f32[1,8,1344]{2,0,1:T(1,128)} %pad_maximum_fusion.7, f32[]{:T(128)} %constant.20.clone.1), padding=0_0_0x0_1_1x0_0_0 | pad | bytes 129028 | tf_op jit(solution)/shard_map/pad | solution.py:97
  153.8 4.7 %pad.154 = f32[1,16,1344]{2,0,1:T(1,128)} pad(f32[1,8,1344]{2,0,1:T(1,128)} %pad_maximum_fusion.6, f32[]{:T(128)} %constant.20.clone.1), padding=0_0_0x0_1_1x0_0_0 | pad | bytes 129028 | tf_op jit(solution)/shard_map/pad | solution.py:97
  158.4 4.7 %pad.155 = f32[1,16,1344]{2,0,1:T(1,128)} pad(f32[1,8,1344]{2,0,1:T(1,128)} %add.512, f32[]{:T(128)} %constant.20.clone.1), padding=0_0_0x1_0_1x0_0_0 | pad | bytes 129028 | tf_op jit(solution)/shard_map/pad | solution.py:97
  163.1 4.7 %pad.165 = f32[1,16,1344]{2,0,1:T(1,128)} pad(f32[1,8,1344]{2,0,1:T(1,128)} %add.519, f32[]{:T(128)} %constant.20.clone.1), padding=0_0_0x1_0_1x0_0_0 | pad | bytes 129028 | tf_op jit(solution)/shard_map/pad | solution.py:97
  169.4 2.0 fusion.34
  172.4 5.6 %pad.307 = f32[1,31,1344]{2,0,1:T(1,128)} pad(f32[1,16,1344]{2,0,1:T(1,128)S(1)} %add.520, f32[]{:T(128)} %constant.20.clone.1), padding=0_0_0x0_0_1x0_0_0 | pad | bytes 252676
  178.0 5.6 %pad.167 = f32[1,32,1344]{2,0,1:T(1,128)} pad(f32[1,16,1344]{2,0,1:T(1,128)S(1)} %add.520, f32[]{:T(128)} %constant.20.clone.1), padding=0_0_0x1_0_1x0_0_0 | pad | bytes 258052 | tf_op jit(solution)/shard_map/pad | solution.py:97
  183.5 8.4 %pad.305 = f32[1,31,1344]{2,0,1:T(1,128)} pad(f32[1,16,1344]{2,0,1:T(1,128)} %add.514, f32[]{:T(128)} %constant.20.clone.1), padding=0_0_0x0_0_1x0_0_0 | pad | bytes 252676
  192.0 8.4 %pad.157 = f32[1,32,1344]{2,0,1:T(1,128)} pad(f32[1,16,1344]{2,0,1:T(1,128)} %add.514, f32[]{:T(128)} %constant.20.clone.1), padding=0_0_0x1_0_1x0_0_0 | pad | bytes 258052 | tf_op jit(solution)/shard_map/pad | solution.py:97
  201.7 5.6 %pad.309 = f32[1,31,1344]{2,0,1:T(1,128)} pad(f32[1,16,1344]{2,0,1:T(1,128)S(1)} %add.486, f32[]{:T(128)} %constant.20.clone.1), padding=0_0_0x0_0_1x0_0_0 | pad | bytes 252676
  207.2 5.5 %pad.137 = f32[1,32,1344]{2,0,1:T(1,128)} pad(f32[1,16,1344]{2,0,1:T(1,128)S(1)} %add.486, f32[]{:T(128)} %constant.20.clone.1), padding=0_0_0x1_0_1x0_0_0 | pad | bytes 258052 | tf_op jit(solution)/shard_map/pad | solution.py:98
  213.7 4.7 %pad.145 = f32[1,16,1344]{2,0,1:T(1,128)} pad(f32[1,8,1344]{2,0,1:T(1,128)} %add.491, f32[]{:T(128)} %constant.20.clone.1), padding=0_0_0x1_0_1x0_0_0 | pad | bytes 129028 | tf_op jit(solution)/shard_map/pad | solution.py:98
  219.4 5.6 %pad.311 = f32[1,31,1344]{2,0,1:T(1,128)} pad(f32[1,16,1344]{2,0,1:T(1,128)S(1)} %add.492, f32[]{:T(128)} %constant.20.clone.1), padding=0_0_0x0_0_1x0_0_0 | pad | bytes 252676
  225.0 5.6 %pad.147 = f32[1,32,1344]{2,0,1:T(1,128)} pad(f32[1,16,1344]{2,0,1:T(1,128)S(1)} %add.492, f32[]{:T(128)} %constant.20.clone.1), padding=0_0_0x1_0_1x0_0_0 | pad | bytes 258052 | tf_op jit(solution)/shard_map/pad | solution.py:98
  231.5 5.6 %pad.156 = f32[1,32,1344]{2,0,1:T(1,128)} pad(f32[1,16,1344]{2,0,1:T(1,128)S(1)} %pad_maximum_fusion.2, f32[]{:T(128)} %constant.20.clone.1), padding=0_0_0x0_1_1x0_0_0 | pad | bytes 258052 | tf_op jit(solution)/shard_map/pad | solution.py:97
  238.1 5.5 %pad.166 = f32[1,32,1344]{2,0,1:T(1,128)} pad(f32[1,16,1344]{2,0,1:T(1,128)S(1)} %pad_maximum_fusion.3, f32[]{:T(128)} %constant.20.clone.1), padding=0_0_0x0_1_1x0_0_0 | pad | bytes 258052 | tf_op jit(solution)/shard_map/pad | solution.py:97
  246.9 8.5 %pad.146 = f32[1,32,1344]{2,0,1:T(1,128)} pad(f32[1,16,1344]{2,0,1:T(1,128)} %pad_maximum_fusion.1, f32[]{:T(128)} %constant.20.clone.1), padding=0_0_0x0_1_1x0_0_0 | pad | bytes 258052 | tf_op jit(solution)/shard_map/pad | solution.py:98
  257.0 8.4 %pad.136 = f32[1,32,1344]{2,0,1:T(1,128)} pad(f32[1,16,1344]{2,0,1:T(1,128)} %pad_maximum_fusion, f32[]{:T(128)} %constant.20.clone.1), padding=0_0_0x0_1_1x0_0_0 | pad | bytes 258052 | tf_op jit(solution)/shard_map/pad | solution.py:98
  269.6 1.9 all_gather.12
  271.6 1.9 all_gather.13
  284.3 7.3 %fusion.15 = (f32[1344]{0:T(1024)}, f32[1,256,1344]{2,1,0:T(8,128)S(1)}, f32[1344]{0:T(1024)}, f32[1344]{0:T(1024)}, f32[1,256,1344]{2,1,0:T(8,128)}) fusion(bf16[1,256,1344]{2,1,0:T(8,128)(2,1)} %copy.78, f32[1,256,1344]{2,1,0:T(8,128)} %copy.77, f32[1344]{0:T(1024)} %param.13, f32[1344]{0:T(1024)S(1)} %fusion.19, f32[1,256,1344]{2,1,0:T(8,128)} %copy.75, ...), kind=kLoop, calls=%fused_computation.84 | loop fusion | flops 15134784 | bytes 10873600 | tf_op jit(solution)/shard_map/reduce_sum | solution.py:125
  294.0 2.2 copy.82
  296.3 2.7 fusion.8
  306.9 3.1 copy.83
  310.0 3.3 add_convert_fusion
  313.3 2.2 copy.84
  315.6 33.0 %all-reduce.44 = (f32[1344]{0:T(1024)}, f32[1344]{0:T(1024)}, f32[1344]{0:T(1024)S(1)}) all-reduce(f32[1344]{0:T(1024)S(1)} %copy-done.35, f32[1344]{0:T(1024)S(1)} %copy-done.34, f32[1344]{0:T(1024)S(1)} %copy-done.36), channel_id=1, replica_groups=mesh['seq'=2,'width'=4,'dp'=4] {'seq','dp'}, use_global_device_ids=true, to_apply=%region_5.6 | all-reduce | flops 4032 | bytes 32256 | tf_op jit(solution)/shard_map/psum | solution.py:127
  349.2 53.6 %all-reduce.48.cloned.1.call-done = (f32[4,336,336]{1,2,0:T(8,128)}, f32[4,336,336]{1,2,0:T(8,128)}) async-done(((f32[4,336,336]{1,2,0:T(8,128)}, f32[4,336,336]{1,2,0:T(8,128)}), (f32[4,336,336]{1,2,0:T(8,128)}, f32[4,336,336]{1,2,0:T(8,128)})) %all-reduce.48.cloned.1.call-update) | async-done | bytes 3612688 | tf_op jit(solution)/shard_map/psum | solution.py:127
  402.8 2.9 copy.85
  405.7 2.9 copy.86
  (208 shorter events, 111.6 us)
Async XLA Ops:
  7.2 8.9 %copy-start = (bf16[4,336,336]{2,1,0:T(8,128)(2,1)S(1)}, bf16[4,336,336]{2,1,0:T(8,128)(2,1)}, u32[]{:S(2)}) copy-start(bf16[4,336,336]{2,1,0:T(8,128)(2,1)} %param.10) | copy-start | bytes 2709508
  7.2 7.3 %copy-start.21 = (bf16[1,256,1344]{1,2,0:T(8,128)(2,1)S(1)}, bf16[1,256,1344]{1,2,0:T(8,128)(2,1)}, u32[]{:S(2)}) copy-start(bf16[1,256,1344]{1,2,0:T(8,128)(2,1)} %param.9) | copy-start | bytes 2064388
  7.2 395.6 %all-reduce.48.cloned.1.call-start = ((), (), s32[]{:S(2)}) async-start(), calls=%async_computation | async-start | bytes 8257536 | tf_op jit(solution)/shard_map/psum | solution.py:127
  8.6 27.3 %collective-permute-start = (s32[1,1]{1,0:T(1,128)}, s32[1,1]{1,0:T(1,128)}, u32[]{:S(2)}, u32[]{:S(2)}) collective-permute-start(s32[1,1]{1,0:T(1,128)} %slice.468), channel_id=1, source_target_pairs={{0,16},{1,17},{2,18},{3,19},{4,20},{5,21},{6,22},{7,23},{8,24},{9,... | collective-permute-start | bytes 20 | tf_op jit(solution)/shard_map/ppermute | solution.py:10
  14.5 1.6 copy-start.6
  16.1 1.2 copy-start.13
  25.0 2.1 copy-start.29
  28.6 7.3 %copy-start.41 = (s32[1,256]{1,0:T(1,128)S(1)}, s32[1,256]{1,0:T(1,128)}, u32[]{:S(2)}) copy-start(s32[1,256]{1,0:T(1,128)} %param.15) | copy-start | bytes 3076
  36.5 9.0 %copy-start.40 = (f32[1,256]{1,0:T(1,128)}, f32[1,256]{1,0:T(1,128)S(1)}, u32[]{:S(2)}) copy-start(f32[1,256]{1,0:T(1,128)S(1)} %get-tuple-element.78) | copy-start | bytes 3076
  37.2 9.1 %copy-start.1 = (f32[1,256,1344]{2,1,0:T(8,128)S(1)}, f32[1,256,1344]{2,1,0:T(8,128)}, u32[]{:S(2)}) copy-start(f32[1,256,1344]{2,1,0:T(8,128)} %copy.77) | copy-start | bytes 4128772
  37.2 9.1 %copy-start.4 = (f32[1,256,1344]{2,1,0:T(8,128)S(1)}, f32[1,256,1344]{2,1,0:T(8,128)}, u32[]{:S(2)}) copy-start(f32[1,256,1344]{2,1,0:T(8,128)} %copy.75) | copy-start | bytes 4128772
  37.2 9.1 %copy-start.31 = (f32[1344]{0:T(1024)S(1)}, f32[1344]{0:T(1024)}, u32[]{:S(2)}) copy-start(f32[1344]{0:T(1024)} %param.13) | copy-start | bytes 16132
  42.0 1.1 copy-start.10
  42.0 4.3 %copy-start.8 = (bf16[1,256,1344]{2,1,0:T(8,128)(2,1)S(1)}, bf16[1,256,1344]{2,1,0:T(8,128)(2,1)}, u32[]{:S(2)}) copy-start(bf16[1,256,1344]{2,1,0:T(8,128)(2,1)} %copy.78) | copy-start | bytes 2064388
  44.8 3.1 copy-start.15
  45.6 2.3 copy-start.42
  63.7 1.1 copy-start.11
  67.5 1.2 copy-start.22
  67.5 1.3 copy-start.23
  68.8 1.2 copy-start.24
  68.8 1.3 copy-start.25
  109.3 1.2 copy-start.26
  109.3 1.3 copy-start.27
  112.5 39.9 %copy-start.39 = (f32[1,1,1344]{2,0,1:T(1,128)S(1)}, f32[1,1,1344]{2,0,1:T(1,128)}, u32[]{:S(2)}) copy-start(f32[1,1,1344]{2,0,1:T(1,128)} %slice.512) | copy-start | bytes 16132
  171.4 30.0 %copy-start.28 = (f32[1,8,1344]{2,0,1:T(1,128)S(1)}, f32[1,8,1344]{2,0,1:T(1,128)}, u32[]{:S(2)}) copy-start(f32[1,8,1344]{2,0,1:T(1,128)} %add.484) | copy-start | bytes 129028
  171.4 41.4 %copy-start.38 = (f32[1,1,1344]{2,0,1:T(1,128)S(1)}, f32[1,1,1344]{2,0,1:T(1,128)}, u32[]{:S(2)}) copy-start(f32[1,1,1344]{2,0,1:T(1,128)} %slice.496) | copy-start | bytes 16132
  218.4 36.9 %slice-start = ((f32[1,32,1344]{2,0,1:T(1,128)}), f32[1,1,1344]{2,0,1:T(1,128)S(1)}, s32[]{:S(2)}) async-start(f32[1,32,1344]{2,0,1:T(1,128)} %copy-done.15), calls=%async_computation.1 | async-start | bytes 11264 | tf_op jit(solution)/shard_map/slice | solution.py:98
  245.4 31.7 %copy-start.17 = (f32[1,32,1344]{2,0,1:T(1,128)S(1)}, f32[1,32,1344]{2,0,1:T(1,128)}, u32[]{:S(2)}) copy-start(f32[1,32,1344]{2,0,1:T(1,128)} %pad.167) | copy-start | bytes 516100
  245.4 32.8 %copy-start.18 = (f32[1,32,1344]{2,0,1:T(1,128)S(1)}, f32[1,32,1344]{2,0,1:T(1,128)}, u32[]{:S(2)}) copy-start(f32[1,32,1344]{2,0,1:T(1,128)} %pad.157) | copy-start | bytes 516100
  268.8 10.9 %copy-start.19 = (f32[1,32,1344]{2,0,1:T(1,128)S(1)}, f32[1,32,1344]{2,0,1:T(1,128)}, u32[]{:S(2)}) copy-start(f32[1,32,1344]{2,0,1:T(1,128)} %pad.147) | copy-start | bytes 516100
  268.8 10.9 %copy-start.20 = (f32[1,32,1344]{2,0,1:T(1,128)S(1)}, f32[1,32,1344]{2,0,1:T(1,128)}, u32[]{:S(2)}) copy-start(f32[1,32,1344]{2,0,1:T(1,128)} %pad.146) | copy-start | bytes 516100
  279.4 4.8 %copy-start.16 = (f32[1,32,1,1344]{3,1,2,0:T(8,128)S(1)}, f32[1,32,1,1344]{3,1,2,0:T(8,128)}, u32[]{:S(2)}) copy-start(f32[1,32,1,1344]{3,1,2,0:T(8,128)} %copy.115) | copy-start | bytes 516100
  279.4 4.8 %copy-start.30 = (f32[1344]{0:T(1024)S(1)}, f32[1344]{0:T(1024)}, u32[]{:S(2)}) copy-start(f32[1344]{0:T(1024)} %param.12) | copy-start | bytes 16132
  284.2 8.5 %copy-start.2 = (f32[1,256,1344]{2,1,0:T(8,128)S(1)}, f32[1,256,1344]{2,1,0:T(8,128)}, u32[]{:S(2)}) copy-start(f32[1,256,1344]{2,1,0:T(8,128)} %copy.77) | copy-start | bytes 4128772
  284.2 8.4 %copy-start.9 = (bf16[1,256,1344]{2,1,0:T(8,128)(2,1)S(1)}, bf16[1,256,1344]{2,1,0:T(8,128)(2,1)}, u32[]{:S(2)}) copy-start(bf16[1,256,1344]{2,1,0:T(8,128)(2,1)} %copy.78) | copy-start | bytes 2064388
  284.2 8.4 %copy-start.32 = (f32[1344]{0:T(1024)S(1)}, f32[1344]{0:T(1024)}, u32[]{:S(2)}) copy-start(f32[1344]{0:T(1024)} %param.13) | copy-start | bytes 16132
  291.5 1.1 copy-start.7
  292.7 3.6 copy-start.5
  298.9 1.4 copy-start.12
  304.1 1.2 copy-start.14
  306.9 3.1 copy-start.3
  306.9 3.1 copy-start.33
  310.0 5.5 %copy-start.34 = (f32[1344]{0:T(1024)S(1)}, f32[1344]{0:T(1024)}, u32[]{:S(2)}) copy-start(f32[1344]{0:T(1024)} %get-tuple-element.75) | copy-start | bytes 16132
  310.0 5.5 %copy-start.35 = (f32[1344]{0:T(1024)S(1)}, f32[1344]{0:T(1024)}, u32[]{:S(2)}) copy-start(f32[1344]{0:T(1024)} %get-tuple-element.80) | copy-start | bytes 16132
  310.0 5.5 %copy-start.36 = (f32[1344]{0:T(1024)S(1)}, f32[1344]{0:T(1024)}, u32[]{:S(2)}) copy-start(f32[1344]{0:T(1024)} %get-tuple-element.81) | copy-start | bytes 16132
  313.3 35.2 %copy-start.37 = (f32[1344]{0:T(1024)S(1)}, f32[1344]{0:T(1024)}, u32[]{:S(2)}) copy-start(f32[1344]{0:T(1024)} %param.14) | copy-start | bytes 16132
Sparse Core Ops, SparseCore 0:
  304.2 98.5 all-reduce.47
where the time goes:
time: 422 us; the launch traced here: 415 us
  local copies, waits for them, and re-layouts  187 us (44%)
  other arithmetic  109 us (26%)
  waiting for transfers between devices  53.7 us (13%)
  blocking collectives  40.5 us (10%)
  between operations  14.7 us (3%)
  matrix products  8.07 us (2%)
    pad x16, local copies, waits for them, and re-layouts, shards(): lax.associative_scan(combine, (group_prod, group_state), axis=1)  64.3 us
    psum x1, waiting for transfers between devices, shards(): lax.psum((local_a, local_x, bias_ga, bias_gx, decay_g), ('seq', 'dp'))  53.6 us
    pad x16, local copies, waits for them, and re-layouts, shards(): lax.associative_scan(combine, (group_prod, group_grad), reverse=True, axi...  53.6 us
    unnamed x98, local copies, waits for them, and re-layouts  41.1 us
    psum x1, blocking collectives, shards(): lax.psum((local_a, local_x, bias_ga, bias_gx, decay_g), ('seq', 'dp'))  33 us
    dot_general x1, other arithmetic, shards(): jnp.einsum('bntsc,bnsc->bntc', factor, drive.reshape(batch, groups, span_...  15.7 us
    add x10, other arithmetic, shards(): lax.associative_scan(combine, (group_prod, group_state), axis=1)  11.8 us
    add x10, other arithmetic, shards(): lax.associative_scan(combine, (group_prod, group_grad), reverse=True, axi...  10.7 us
  transfers between devices with their start and end apart: 2, of which 1 were waited for; matrix products, arithmetic and copies ran while one was open for 8% of the time, Pallas kernels for 0%

commit v1 on v0

--- a/solution.py
+++ b/solution.py
@@ -1,7 +1,16 @@
+import functools
+
 import jax
 import jax.numpy as jnp
 from jax import lax
+from jax.experimental import pallas as pl
+from jax.experimental.pallas import tpu as pltpu
 from jax.sharding import PartitionSpec as P
+
+LANES = 128
+ROWS = 8
+F32 = jnp.float32
+BF16 = jnp.bfloat16
 
 
 def shifted(value, axis, steps):
@@ -31,7 +40,7 @@
     return (earlier[0] * later[0], earlier[1] * later[0] + later[1])
 
 
-def shards(inputs, out_grad, gate_a, gate_x, bias_a, bias_x, decay_param, segment_ids):
+def general(inputs, out_grad, gate_a, gate_x, bias_a, bias_x, decay_param, segment_ids):
     batch, count, chans = inputs.shape
     blocks, width_k = (gate_a.shape[0], gate_a.shape[1])
     span_len = 8
@@ -130,6 +139,317 @@
     return (input_grad, grad_a, grad_x, bias_ga, bias_gx, jax.nn.sigmoid(decay_param) * decay_g)
 
 
+def minus_expm1(value, exp_value):
+    series = 1.0 + value * (1.0 / 8.0)
+    for term in (7, 6, 5, 4, 3, 2):
+        series = 1.0 + value * (1.0 / term) * series
+    return jnp.where(value > -0.25, -value * series, 1.0 - exp_value)
+
+
+def block_kernel(
+    core_ref, own_x, own_dy, other, own_seg, wa_ref, wx_ref, ba_ref, bx_ref, soft_ref,
+    ga_ref, gx_ref, ig_own, ig_other,
+    x_s, seg_s, ab_s, u_s, dy_s, r_s, k2_s, k3_s, mi_s, da_s, dx_s,
+):
+    count, width = own_x.shape
+    total = 2 * count
+    core = core_ref[0]
+    mine = pl.ds(pl.multiple_of(core * count, count), count)
+    theirs = pl.ds(pl.multiple_of((1 - core) * count, count), count)
+    x_s[mine, :] = own_x[...]
+    x_s[theirs, :] = other[0, :, :width].astype(BF16)
+    seg_s[pl.ds(pl.multiple_of(ROWS + core * count, ROWS), count), :] = own_seg[...]
+    seg_s[pl.ds(pl.multiple_of(ROWS + (1 - core) * count, ROWS), count), :] = other[2, :, :LANES]
+    seg_s[:ROWS, :] = jnp.zeros((ROWS, LANES), F32)
+
+    wa = wa_ref[0]
+    wx = wx_ref[0]
+    ba = ba_ref[0]
+    bx = bx_ref[0]
+    soft = soft_ref[0]
+    tiles = -(-width // LANES)
+    piece = 128
+    edges = [(t * LANES, min(width, (t + 1) * LANES)) for t in range(tiles)]
+
+    def put(ref, rows, value):
+        for tile, (low, high) in enumerate(edges):
+            ref[tile, rows, : high - low] = value[:, low:high]
+
+    def get(ref, rows):
+        return jnp.concatenate([ref[tile, rows, :] for tile in range(tiles)], 1)[:, :width]
+
+    put(dy_s, mine, own_dy[...].astype(F32))
+    put(dy_s, theirs, other[1, :, :width])
+
+    def gates(step, _):
+        base = pl.multiple_of(step * piece, piece)
+        rows = pl.ds(base, piece)
+        xb = x_s[rows, :]
+        xf = xb.astype(F32)
+        rate = jax.nn.sigmoid(jnp.dot(xb, wa, preferred_element_type=F32) + ba)
+        ingate = jax.nn.sigmoid(jnp.dot(xb, wx, preferred_element_type=F32) + bx)
+        log_a = -8.0 * rate * soft
+        decay = jnp.exp(log_a)
+        seg = seg_s[pl.ds(pl.multiple_of(ROWS + base, ROWS), piece), :]
+        seg_prev = seg_s[pl.ds(ROWS - 1 + base, piece), :]
+        place = base + lax.broadcasted_iota(jnp.int32, (piece, LANES), 0)
+        keep1 = jnp.where((seg != seg_prev) | (place == 0), 0.0, 1.0)
+        keep = jnp.concatenate([keep1] * tiles, 1)[:, :width]
+        two = 2.0 * log_a
+        power = jnp.maximum(minus_expm1(two, decay * decay), 1e-37)
+        inv = lax.rsqrt(power)
+        mult = jnp.where(keep > 0.5, power * inv, 1.0)
+        mi = mult * ingate
+        put(ab_s, rows, keep * decay)
+        put(u_s, rows, mi * xf)
+        r_s[rows, :] = rate
+        k2_s[rows, :] = ingate * xf * decay * inv
+        k3_s[rows, :] = xf * (1.0 - ingate)
+        mi_s[rows, :] = mi
+        return 0
+
+    lax.fori_loop(0, total // piece, gates, 0)
+
+    steps = total // ROWS
+    every = range(tiles)
+
+    def at(step):
+        return pl.ds(step, ROWS, stride=steps)
+
+    zero = jnp.zeros((ROWS, LANES), F32)
+
+    def ends(step, carry):
+        late = steps - 1 - step
+        out = []
+        for tile, (state, prod, back) in zip(every, carry):
+            decay = ab_s[tile, at(step), :]
+            state = decay * state + u_s[tile, at(step), :]
+            back = ab_s[tile, at(late), :] * (dy_s[tile, at(late), :] + back)
+            out.append((state, decay * prod, back))
+        return out
+
+    found = lax.fori_loop(0, steps, ends, [(zero, zero + 1.0, zero)] * tiles, unroll=8)
+    entering = []
+    for state, prod, back in found:
+        run = jnp.zeros((1, LANES), F32)
+        firsts = []
+        for row in range(ROWS):
+            firsts.append(run)
+            run = state[row : row + 1] + prod[row : row + 1] * run
+        run = jnp.zeros((1, LANES), F32)
+        lasts = []
+        for row in reversed(range(ROWS)):
+            lasts.append(run)
+            run = back[row : row + 1] + prod[row : row + 1] * run
+        entering.append((jnp.concatenate(firsts, 0), jnp.concatenate(lasts[::-1], 0)))
+
+    def scan(step, carry):
+        late = steps - 1 - step
+        out = []
+        for tile, (state, back) in zip(every, carry):
+            drive = u_s[tile, at(step), :]
+            u_s[tile, at(step), :] = state
+            state = ab_s[tile, at(step), :] * state + drive
+            grad = dy_s[tile, at(late), :] + back
+            dy_s[tile, at(late), :] = grad
+            out.append((state, ab_s[tile, at(late), :] * grad))
+        return out
+
+    lax.fori_loop(0, steps, scan, entering, unroll=8)
+    zero = jnp.zeros((ROWS, width), F32)
+
+    def gradients(step, sums):
+        rows = pl.ds(pl.multiple_of(step * piece, piece), piece)
+        grad = get(dy_s, rows)
+        rate = r_s[rows, :]
+        q = -8.0 * rate * get(ab_s, rows) * grad * (get(u_s, rows) - k2_s[rows, :])
+        dpre_a = soft * (1.0 - rate) * q
+        direct = grad * mi_s[rows, :]
+        dpre_x = direct * k3_s[rows, :]
+        put(dy_s, rows, direct)
+        da_s[rows, :] = dpre_a.astype(BF16)
+        dx_s[rows, :] = dpre_x.astype(BF16)
+        shape = (piece // ROWS, ROWS, width)
+        return tuple(
+            acc + jnp.sum(v.reshape(shape), 0) for acc, v in zip(sums, (dpre_a, q, dpre_x))
+        )
+
+    sum_a, sum_q, sum_x = lax.fori_loop(0, total // piece, gradients, (zero, zero, zero))
+    row_id = lax.broadcasted_iota(jnp.int32, (ROWS, width), 0)
+    across = (((0,), (0,)), ((), ()))
+    x_all = x_s[...]
+    ga_ref[:width, :] = lax.dot_general(x_all, da_s[...], across, preferred_element_type=F32)
+    gx_ref[:width, :] = lax.dot_general(x_all, dx_s[...], across, preferred_element_type=F32)
+    tot_a = jnp.sum(sum_a, 0, keepdims=True)
+    tot_q = jnp.sum(sum_q, 0, keepdims=True)
+    tot_x = jnp.sum(sum_x, 0, keepdims=True)
+    ga_ref[width:, :] = jnp.where(row_id == 0, tot_a, jnp.where(row_id == 1, tot_q, 0.0))
+    gx_ref[width:, :] = jnp.where(row_id == 0, tot_x, 0.0)
+    along = (((1,), (1,)), ((), ()))
+
+    def returned(where):
+        back = lax.dot_general(da_s[where, :], wa, along, preferred_element_type=F32)
+        back += lax.dot_general(dx_s[where, :], wx, along, preferred_element_type=F32)
+        return get(dy_s, where) + back
+
+    ig_other[...] = returned(theirs)
+    ig_own[...] = returned(mine)
+
+
+def run_block(which, core, own_x, own_dy, other, own_seg, gate_a, gate_x, bias_a, bias_x, soft):
+    count, width = own_x.shape
+    blocks = gate_a.shape[0]
+    per_core = blocks // 2
+    total = 2 * count
+
+    def whole(shape):
+        return pl.BlockSpec(shape, lambda i, c: (0,) * len(shape))
+
+    def picked(rows):
+        return pl.BlockSpec((1, rows, width), lambda i, c: (per_core * c[0] + which, 0, 0))
+
+    f32 = functools.partial(pltpu.VMEM, dtype=F32)
+    wide = (total, width)
+    tiled = (-(-width // LANES), total, LANES)
+    return pl.pallas_call(
+        block_kernel,
+        grid_spec=pltpu.PrefetchScalarGridSpec(
+            num_scalar_prefetch=1,
+            grid=(1,),
+            in_specs=[
+                whole(own_x.shape), whole(own_dy.shape), whole(other.shape), whole(own_seg.shape),
+                picked(width), picked(width), picked(1), picked(1), picked(1),
+            ],
+            out_specs=[
+                whole((width + ROWS, width)), whole((width + ROWS, width)),
+                whole((count, width)), whole((count, width)),
+            ],
+            scratch_shapes=[
+                pltpu.VMEM(wide, BF16), f32((total + ROWS, LANES)), f32(tiled), f32(tiled), f32(tiled),
+                f32(wide), f32(wide), f32(wide), f32(wide), pltpu.VMEM(wide, BF16), pltpu.VMEM(wide, BF16),
+            ],
+        ),
+        out_shape=[
+            jax.ShapeDtypeStruct((width + ROWS, width), F32),
+            jax.ShapeDtypeStruct((width + ROWS, width), F32),
+            jax.ShapeDtypeStruct((count, width), F32),
+            jax.ShapeDtypeStruct((count, width), F32),
+        ],
+        cost_estimate=pl.CostEstimate(
+            flops=12 * total * width * width, bytes_accessed=8 * total * width, transcendentals=6 * total * width
+        ),
+    )(core, own_x, own_dy, other, own_seg, gate_a, gate_x, bias_a, bias_x, soft)
+
+
+def join_kernel(core_ref, *refs):
+    out_ref = refs[-1]
+    half = len(refs) // 2
+    for core in range(2):
+        order = refs[:half] + refs[half:-1] if core == 0 else refs[half:-1] + refs[:half]
+
+        @pl.when(core_ref[0] == core)
+        def _(order=order):
+            out_ref[...] = jnp.concatenate([ref[...] for ref in order], 1).astype(BF16)
+
+
+def join_columns(core, own, theirs):
+    count, width = own[0].shape
+    parts = own + theirs
+    return pl.pallas_call(
+        join_kernel,
+        in_specs=[pl.BlockSpec(memory_space=pltpu.SMEM)] + [pl.BlockSpec(memory_space=pltpu.VMEM)] * len(parts),
+        out_specs=pl.BlockSpec(memory_space=pltpu.VMEM),
+        out_shape=jax.ShapeDtypeStruct((count, width * len(parts)), BF16),
+        cost_estimate=pl.CostEstimate(
+            flops=count * width * len(parts), bytes_accessed=6 * count * width * len(parts), transcendentals=0
+        ),
+    )(core, *parts)
+
+
+def line_sum(value, axis):
+    size = lax.axis_size(axis)
+    if size == 1:
+        return value
+    if size % 2:
+        return lax.psum(value, axis)
+    me = lax.axis_index(axis)
+    half = size // 2
+    for hop in range(half - 1):
+        value = value + lax.ppermute(value, axis, [(hop, hop + 1), (size - 1 - hop, size - 2 - hop)])
+    value = value + lax.ppermute(value, axis, [(half - 1, half), (half, half - 1)])
+    for hop in reversed(range(half - 1)):
+        came = lax.ppermute(value, axis, [(hop + 1, hop), (size - 2 - hop, size - 1 - hop)])
+        value = jnp.where((me == hop) | (me == size - 1 - hop), came, value)
+    return value
+
+
+def paired(inputs, out_grad, gate_a, gate_x, bias_a, bias_x, decay_param, segment_ids):
+    count, chans = inputs.shape[1:]
+    blocks, width = gate_a.shape[:2]
+    per_core = blocks // 2
+    half = chans // 2
+    core = lax.axis_index("seq")
+    first = core == 0
+    swap = [(0, 1), (1, 0)]
+    padded = (width // LANES + 1) * LANES
+
+    def halves(value):
+        low, high = value[:, :half], value[:, half:]
+        return jnp.where(first, low, high), jnp.where(first, high, low)
+
+    own_x, out_x = halves(inputs[0])
+    own_dy, out_dy = halves(out_grad[0])
+    seg = jnp.broadcast_to(segment_ids[0].astype(F32)[:, None], (count, LANES))
+    core_arr = core.astype(jnp.int32).reshape(1)
+    bias_a3, bias_x3 = bias_a.reshape(blocks, 1, width), bias_x.reshape(blocks, 1, width)
+    soft3 = jax.nn.softplus(decay_param).reshape(blocks, 1, width)
+
+    def cols(value, which):
+        return value[:, which * width : (which + 1) * width]
+
+    def widen(value):
+        return jnp.pad(value.astype(F32), ((0, 0), (0, padded - value.shape[1])))
+
+    others = []
+    for which in range(per_core):
+        sent = jnp.stack([widen(cols(out_x, which)), widen(cols(out_dy, which)), widen(seg)])
+        others.append(lax.ppermute(sent, "seq", swap))
+    own_ig, their_ig, totals = [], [], []
+    for which in range(per_core):
+        ga, gx, mine, theirs = run_block(
+            which, core_arr, cols(own_x, which), cols(own_dy, which), others[which], seg,
+            gate_a, gate_x, bias_a3, bias_x3, soft3,
+        )
+        own_ig.append(mine)
+        their_ig.append(lax.ppermute(theirs, "seq", swap))
+        totals.append([line_sum(ga, "dp"), line_sum(gx, "dp")])
+    fetched = [[lax.ppermute(part, "seq", swap) for part in pair] for pair in totals]
+
+    def ordered(mine, theirs, join):
+        return jnp.where(first, join(mine + theirs), join(theirs + mine))
+
+    input_grad = join_columns(core_arr, own_ig, their_ig)[None]
+    whole_a = ordered([t[0] for t in totals], [t[0] for t in fetched], jnp.stack)
+    whole_x = ordered([t[1] for t in totals], [t[1] for t in fetched], jnp.stack)
+    return (
+        input_grad,
+        whole_a[:, :width],
+        whole_x[:, :width],
+        whole_a[:, width].reshape(chans),
+        whole_x[:, width].reshape(chans),
+        jax.nn.sigmoid(decay_param) * whole_a[:, width + 1].reshape(chans),
+    )
+
+
+def shards(inputs, out_grad, gate_a, gate_x, bias_a, bias_x, decay_param, segment_ids):
+    batch, count, _ = inputs.shape
+    if lax.axis_size("seq") == 2 and batch == 1 and gate_a.shape[0] % 2 == 0 and count % 128 == 0:
+        body = paired
+    else:
+        body = general
+    return body(inputs, out_grad, gate_a, gate_x, bias_a, bias_x, decay_param, segment_ids)
+
+
 def solution(mesh):
     in_specs = (
         P("dp", "seq", "width"),

time: 422 us -> 155 us (0.37); the launches traced: 415 us -> 153 us
  local copies, waits for them, and re-layouts: 187 us -> 53.6 us
  other arithmetic: 109 us -> 6.08 us
  blocking collectives: 40.5 us -> 0 us
  Pallas kernels: 0 us -> 25.3 us
  starting transfers between devices: 2.94 us -> 23.1 us
  between operations: 14.7 us -> 1.09 us
  waiting for transfers between devices: 53.7 us -> 44.2 us
  matrix products: 8.07 us -> 0 us
    pad x32 -> x0, local copies, waits for them, and re-layouts: 118 us -> none  [the longest x16 64.3 us: shards(): lax.associative_scan(combine, (group_prod, group_state), axis=1)]
    psum x1 -> x0, waiting for transfers between devices: 53.6 us -> none  [shards(): lax.psum((local_a, local_x, bias_ga, bias_gx, decay_g), ('seq', 'dp'))]
    ppermute x1 -> x20, waiting for transfers between devices: 0.01 us -> 44.2 us  [the longest x4 30.6 us: line_sum(): lax.ppermute(value, axis, [(hop + 1, hop), (size - 2 - hop, size - 1 - ho...]
    unnamed x98 -> x27, local copies, waits for them, and re-layouts: 41.1 us -> 5.87 us
    add x35 -> x8, other arithmetic: 34.1 us -> 0.52 us  [the longest x4 0.26 us: line_sum(): value + lax.ppermute(value, axis, [(half - 1, half), (half, half - 1)])]
    psum x1 -> x0, blocking collectives: 33 us -> none  [shards(): lax.psum((local_a, local_x, bias_ga, bias_gx, decay_g), ('seq', 'dp'))]
    pallas_call x0 -> x3, Pallas kernels: none -> 25.3 us  [the longest x2 22.8 us: run_block(): pl.pallas_call(block_kernel, grid_spec=pltpu.PrefetchScalarGridSpec(num_s...]
    dot_general x2 -> x0, other arithmetic: 20.5 us -> none  [the longest x1 15.7 us: shards(): jnp.einsum('bntsc,bnsc->bntc', factor, drive.reshape(batch, groups, span_...]
  transfers between devices with their start and end apart: 2 -> 20, of which waited for: 1 -> 7; matrix products, arithmetic and copies ran while one was open for 8% -> 29% of each run, Pallas kernels for 0% -> 16%
where the time goes in v1:
time: 155 us; the launch traced here: 153 us
  local copies, waits for them, and re-layouts  53.6 us (35%)
  waiting for transfers between devices  44.2 us (29%)
  Pallas kernels  25.3 us (16%)
  starting transfers between devices  23.1 us (15%)
  other arithmetic  6.08 us (4%)
    ppermute x4, waiting for transfers between devices, line_sum(): lax.ppermute(value, axis, [(hop + 1, hop), (size - 2 - hop, size - 1 - ho...  30.6 us
    pallas_call x2, Pallas kernels, run_block(): pl.pallas_call(block_kernel, grid_spec=pltpu.PrefetchScalarGridSpec(num_s...  22.8 us
    ppermute x4, waiting for transfers between devices, line_sum(): lax.ppermute(value, axis, [(hop, hop + 1), (size - 1 - hop, size - 2 - ho...  11.5 us
    ppermute x4, starting transfers between devices, line_sum(): lax.ppermute(value, axis, [(hop, hop + 1), (size - 1 - hop, size - 2 - ho...  10.6 us
    pallas_call x4, local copies, waits for them, and re-layouts, run_block(): pl.pallas_call(block_kernel, grid_spec=pltpu.PrefetchScalarGridSpec(num_s...  7.52 us
    ppermute x4, local copies, waits for them, and re-layouts, paired(): lax.ppermute(part, 'seq', swap)  6.63 us
    ppermute x4, starting transfers between devices, line_sum(): lax.ppermute(value, axis, [(half - 1, half), (half, half - 1)])  6.09 us
    unnamed x27, local copies, waits for them, and re-layouts  5.87 us
  transfers between devices with their start and end apart: 20, of which 7 were waited for; matrix products, arithmetic and copies ran while one was open for 29% of the time, Pallas kernels for 16%

profile of v1, /device:TPU:0, one launch (start us, length us, event | category | flops | bytes accessed | tf_op | source)
XLA Modules:
  0.0 153.3 jit_solution(4146721054662929432)
XLA Ops:
  1.5 1.5 copy.17
  4.2 1.6 %pad_maximum_fusion = (f32[3,256,384]{2,1,0:T(8,128)}, f32[3,256,384]{2,1,0:T(8,128)}) fusion(f32[1,256,384]{2,1,0:T(8,128)S(1)} %pad_bitcast_fusion, f32[1,256,384]{2,1,0:T(8,128)S(1)} %bitcast_convert_fusion, f32[1,256,384]{2,1,0:T(8,128)S(1)} %bitcast_convert_fusion.1, f32[1,256,384]{2,1,0:T(8,128)S(1)} %get-tuple-element.47, ...), kind=kLoop, calls=%fused_computation.2 | loop fusion | flops 1179648 | bytes 4325376 | tf_op jit(solution)/shard_map/stack | solution.py:415
  10.0 11.4 %shard_map.128 = (f32[344,336]{1,0:T(8,128)}, f32[344,336]{1,0:T(8,128)}, f32[256,336]{1,0:T(8,128)}, f32[256,336]{1,0:T(8,128)}) custom-call(s32[1]{0:T(128)} %bitcast.core_ref, bf16[256,336]{1,0:T(8,128)(2,1)} %get-tuple-element.44.own_x, bf16[256,336]{1,0:T(8,128)(2,1)} %get-tuple-element.42.own_dy, f32[3,256,384]{2,1,0:T(8,128)} %collective-permute-done.1.other, ...), custom_call_target="tpu_custom_call" | custom-call | flops 693633024 | bytes 1376256 | tf_op jit(solution)/shard_map/pallas_call | solution.py:314
  21.4 2.1 %copy.41 = f32[344,336]{0,1:T(8,128)} copy(f32[344,336]{1,0:T(8,128)} %get-tuple-element.21) | data formatting | bytes 924672 | tf_op jit(solution)/shard_map/pallas_call | solution.py:314
  23.5 5.0 %collective-permute-start.15 = (f32[344,336]{0,1:T(8,128)}, f32[344,336]{0,1:T(8,128)S(1)}, u32[]{:S(2)}, u32[]{:S(2)}) collective-permute-start(f32[344,336]{0,1:T(8,128)} %copy.41), channel_id=1, source_target_pairs={{0,1},{3,2},{4,5},{7,6},{8,9},{11,10},{12,13},{15,14},{16,17},{19,... | collective-permute-start | bytes 1387016 | tf_op jit(solution)/shard_map/ppermute | solution.py:378
  28.5 1.3 copy.25
  29.7 1.3 collective-permute-start.7
  32.1 11.4 %shard_map.127 = (f32[344,336]{1,0:T(8,128)}, f32[344,336]{1,0:T(8,128)}, f32[256,336]{1,0:T(8,128)}, f32[256,336]{1,0:T(8,128)}) custom-call(s32[1]{0:T(128)} %bitcast.core_ref, bf16[256,336]{1,0:T(8,128)(2,1)} %get-tuple-element.45.own_x, bf16[256,336]{1,0:T(8,128)(2,1)} %get-tuple-element.43.own_dy, f32[3,256,384]{2,1,0:T(8,128)} %copy-done.5, ...), custom_call_target="tpu_custom_call" | custom-call | flops 693633024 | bytes 1376256 | tf_op jit(solution)/shard_map/pallas_call | solution.py:314
  43.5 2.1 %copy.35 = f32[344,336]{0,1:T(8,128)} copy(f32[344,336]{1,0:T(8,128)} %get-tuple-element.20) | data formatting | bytes 924672 | tf_op jit(solution)/shard_map/pallas_call | solution.py:314
  45.6 2.1 %collective-permute-start.12 = (f32[344,336]{0,1:T(8,128)}, f32[344,336]{0,1:T(8,128)}, u32[]{:S(2)}, u32[]{:S(2)}) collective-permute-start(f32[344,336]{0,1:T(8,128)} %copy.35), channel_id=1, source_target_pairs={{0,1},{3,2},{4,5},{7,6},{8,9},{11,10},{12,13},{15,14},{16,17},{19,... | collective-permute-start | bytes 1387016 | tf_op jit(solution)/shard_map/ppermute | solution.py:378
  47.7 2.0 %copy.19 = f32[344,336]{0,1:T(8,128)} copy(f32[344,336]{1,0:T(8,128)} %get-tuple-element.18) | data formatting | bytes 924672 | tf_op jit(solution)/shard_map/pallas_call | solution.py:314
  49.8 2.2 %collective-permute-start.4 = (f32[344,336]{0,1:T(8,128)}, f32[344,336]{0,1:T(8,128)}, u32[]{:S(2)}, u32[]{:S(2)}) collective-permute-start(f32[344,336]{0,1:T(8,128)} %copy.19), channel_id=1, source_target_pairs={{0,1},{3,2},{4,5},{7,6},{8,9},{11,10},{12,13},{15,14},{16,17},{19,... | collective-permute-start | bytes 1387016 | tf_op jit(solution)/shard_map/ppermute | solution.py:378
  52.3 1.0 copy.43
  53.3 1.6 %collective-permute-start.16 = (f32[344,336]{0,1:T(8,128)}, f32[344,336]{0,1:T(8,128)}, u32[]{:S(2)}, u32[]{:S(2)}) collective-permute-start(f32[344,336]{0,1:T(8,128)} %copy.43), channel_id=1, source_target_pairs={{1,2},{2,1},{5,6},{6,5},{9,10},{10,9},{13,14},{14,13},{17,18},{18,... | collective-permute-start | bytes 1387016 | tf_op jit(solution)/shard_map/ppermute | solution.py:379
  56.2 1.6 %collective-permute-start.8 = (f32[344,336]{0,1:T(8,128)}, f32[344,336]{0,1:T(8,128)}, u32[]{:S(2)}, u32[]{:S(2)}) collective-permute-start(f32[344,336]{0,1:T(8,128)} %copy.27), channel_id=1, source_target_pairs={{1,2},{2,1},{5,6},{6,5},{9,10},{10,9},{13,14},{14,13},{17,18},{18,... | collective-permute-start | bytes 1387016 | tf_op jit(solution)/shard_map/ppermute | solution.py:379
  57.8 5.2 %collective-permute-done.12 = f32[344,336]{0,1:T(8,128)} collective-permute-done((f32[344,336]{0,1:T(8,128)}, f32[344,336]{0,1:T(8,128)}, u32[]{:S(2)}, u32[]{:S(2)}) %collective-permute-start.12) | collective-permute-done | bytes 462368 | tf_op jit(solution)/shard_map/ppermute | solution.py:378
  63.0 1.3 copy.36
  64.3 1.0 copy.37
  65.4 1.5 collective-permute-start.13
  66.8 6.3 %collective-permute-done.4 = f32[344,336]{0,1:T(8,128)} collective-permute-done((f32[344,336]{0,1:T(8,128)}, f32[344,336]{0,1:T(8,128)}, u32[]{:S(2)}, u32[]{:S(2)}) %collective-permute-start.4) | collective-permute-done | bytes 462368 | tf_op jit(solution)/shard_map/ppermute | solution.py:378
  73.1 1.3 copy.20
  75.4 1.5 collective-permute-start.5
  76.9 1.3 copy.44
  79.3 1.3 collective-permute-start.17
  80.6 1.3 copy.28
  82.9 1.3 collective-permute-start.9
  84.3 1.3 copy.38
  86.6 1.5 collective-permute-start.14
  88.1 1.3 copy.22
  90.4 1.3 collective-permute-start.6
  91.7 6.2 %collective-permute-done.17 = f32[344,336]{0,1:T(8,128)} collective-permute-done((f32[344,336]{0,1:T(8,128)}, f32[344,336]{0,1:T(8,128)}, u32[]{:S(2)}, u32[]{:S(2)}) %collective-permute-start.17) | collective-permute-done | bytes 462368 | tf_op jit(solution)/shard_map/ppermute | solution.py:381
  98.0 1.3 copy.46
  100.3 8.7 %collective-permute-done.9 = f32[344,336]{0,1:T(8,128)} collective-permute-done((f32[344,336]{0,1:T(8,128)}, f32[344,336]{0,1:T(8,128)}, u32[]{:S(2)}, u32[]{:S(2)}) %collective-permute-start.9) | collective-permute-done | bytes 462368 | tf_op jit(solution)/shard_map/ppermute | solution.py:381
  109.0 1.3 copy.30
  111.4 8.7 %collective-permute-done.14 = f32[344,336]{0,1:T(8,128)} collective-permute-done((f32[344,336]{0,1:T(8,128)}, f32[344,336]{0,1:T(8,128)}, u32[]{:S(2)}, u32[]{:S(2)}) %collective-permute-start.14) | collective-permute-done | bytes 462368 | tf_op jit(solution)/shard_map/ppermute | solution.py:381
  120.1 1.3 copy.40
  122.4 6.9 %collective-permute-done.6 = f32[344,336]{0,1:T(8,128)} collective-permute-done((f32[344,336]{0,1:T(8,128)}, f32[344,336]{0,1:T(8,128)}, u32[]{:S(2)}, u32[]{:S(2)}) %collective-permute-start.6) | collective-permute-done | bytes 462368 | tf_op jit(solution)/shard_map/ppermute | solution.py:381
  129.3 1.3 copy.24
  132.2 2.2 %collective-permute-done.2.refs_2_ = f32[256,336]{1,0:T(8,128)S(1)} collective-permute-done((f32[256,336]{1,0:T(8,128)}, f32[256,336]{1,0:T(8,128)S(1)}, u32[]{:S(2)}, u32[]{:S(2)}) %collective-permute-start.2) | collective-permute-done | bytes 344096 | tf_op jit(solution)/shard_map/ppermute | solution.py:424
  135.1 2.4 %shard_map.129 = bf16[256,1344]{1,0:T(8,128)(2,1)} custom-call(s32[1]{0:T(128)} %bitcast.core_ref, f32[256,336]{1,0:T(8,128)} %get-tuple-element.14.refs_0_, f32[256,336]{1,0:T(8,128)} %get-tuple-element.15.refs_1_, f32[256,336]{1,0:T(8,128)} %copy-done.7, f32[256,336]{1,0:T(8,128)} %collective-permute-done.3.refs_3_), custom_call_target="tpu_custom_call" | custom-call | flops 344064 | bytes 2064384 | tf_op jit(solution)/shard_map/pallas_call | solution.py:358
  137.5 2.2 %copy.51 = bf16[1,256,1344]{1,2,0:T(8,128)(2,1)} copy(bf16[1,256,1344]{2,1,0:T(8,128)(2,1)} %bitcast.37) | data formatting | bytes 1376256
  139.7 1.3 copy.50
  141.0 1.3 copy.34
  142.3 2.1 %copy.48 = f32[344,336]{1,0:T(8,128)} copy(f32[344,336]{0,1:T(8,128)} %collective-permute-done.18) | data formatting | bytes 924672 | tf_op jit(solution)/shard_map/ppermute | solution.py:426
  144.3 2.1 %copy.32 = f32[344,336]{1,0:T(8,128)} copy(f32[344,336]{0,1:T(8,128)} %collective-permute-done.10) | data formatting | bytes 924672 | tf_op jit(solution)/shard_map/ppermute | solution.py:426
  146.4 1.9 %maximum_select_fusion = (f32[4,344,336]{2,1,0:T(8,128)S(1)}, f32[4,344,336]{2,1,0:T(8,128)S(1)}) fusion(f32[1,344,336]{2,1,0:T(8,128)S(1)} %bitcast.39, f32[1,344,336]{2,1,0:T(8,128)} %bitcast.41, f32[1,344,336]{2,1,0:T(8,128)S(1)} %bitcast.32, f32[1,344,336]{2,1,0:T(8,128)S(1)} %bitcast.34, pred[]{:T(512)S(6)} %eq.6, f32[1,344,336]{2,1,0:T(8,128)S(1)} %bitcast.31, ...), kind=kLoop, calls=%fused_computation | loop fusion | flops 6472704 | bytes 7397377 | tf_op jit(solution)/shard_map/jit(_where)/select_n | solution.py:429
  148.4 1.4 slice.83
  149.8 1.4 slice.82
  (92 shorter events, 21.9 us)
Async XLA Ops:
  1.4 1.9 %copy-start.4 = (f32[256,128]{1,0:T(8,128)}, f32[256,128]{1,0:T(8,128)S(1)}, u32[]{:S(2)}) copy-start(f32[256,128]{1,0:T(8,128)S(1)} %broadcast_in_dim.4.own_seg) | copy-start | bytes 393220
  1.5 1.9 %copy-start.6 = (bf16[1,256,1344]{1,2,0:T(8,128)(2,1)S(1)}, bf16[1,256,1344]{1,2,0:T(8,128)(2,1)}, u32[]{:S(2)}) copy-start(bf16[1,256,1344]{1,2,0:T(8,128)(2,1)} %param.9) | copy-start | bytes 2064388
  3.2 0.9 copy-start.11
  4.1 2.1 %copy-start.9 = (f32[1344]{0:T(1024)S(1)}, f32[1344]{0:T(1024)}, u32[]{:S(2)}) copy-start(f32[1344]{0:T(1024)} %param.12) | copy-start | bytes 16132
  4.1 2.8 %copy-start.10 = (f32[1344]{0:T(1024)S(1)}, f32[1344]{0:T(1024)}, u32[]{:S(2)}) copy-start(f32[1344]{0:T(1024)} %param.13) | copy-start | bytes 16132
  4.2 3.5 %copy-start.8 = (f32[1344]{0:T(1024)S(1)}, f32[1344]{0:T(1024)}, u32[]{:S(2)}) copy-start(f32[1344]{0:T(1024)} %param.14) | copy-start | bytes 16132
  5.7 4.2 %collective-permute-start.1 = (f32[3,256,384]{2,1,0:T(8,128)}, f32[3,256,384]{2,1,0:T(8,128)}, u32[]{:S(2)}, u32[]{:S(2)}) collective-permute-start(f32[3,256,384]{2,1,0:T(8,128)} %get-tuple-element.40), channel_id=1, source_target_pairs={{0,16},{16,0},{1,17},{17,1},{2,18},{18,2},{3,19},{19,3},{4,20},{20... | collective-permute-start | bytes 3538952 | tf_op jit(solution)/shard_map/ppermute | solution.py:416
  6.2 24.8 %collective-permute-start = (f32[3,256,384]{2,1,0:T(8,128)}, f32[3,256,384]{2,1,0:T(8,128)S(1)}, u32[]{:S(2)}, u32[]{:S(2)}) collective-permute-start(f32[3,256,384]{2,1,0:T(8,128)} %get-tuple-element.41), channel_id=1, source_target_pairs={{0,16},{16,0},{1,17},{17,1},{2,18},{18,2},{3,19},{19,3},{4,20},{20... | collective-permute-start | bytes 3538952 | tf_op jit(solution)/shard_map/ppermute | solution.py:416
  23.5 28.5 %collective-permute-start.15 = (f32[344,336]{0,1:T(8,128)}, f32[344,336]{0,1:T(8,128)S(1)}, u32[]{:S(2)}, u32[]{:S(2)}) collective-permute-start(f32[344,336]{0,1:T(8,128)} %copy.41), channel_id=1, source_target_pairs={{0,1},{3,2},{4,5},{7,6},{8,9},{11,10},{12,13},{15,14},{16,17},{19,... | collective-permute-start | bytes 1387016 | tf_op jit(solution)/shard_map/ppermute | solution.py:378
  29.7 25.2 %collective-permute-start.7 = (f32[344,336]{0,1:T(8,128)S(1)}, f32[344,336]{0,1:T(8,128)S(1)}, u32[]{:S(2)}, u32[]{:S(2)}) collective-permute-start(f32[344,336]{0,1:T(8,128)S(1)} %copy.25), channel_id=1, source_target_pairs={{0,1},{3,2},{4,5},{7,6},{8,9},{11,10},{12,13},{15,14},{16,17},{19,... | collective-permute-start | bytes 1387016 | tf_op jit(solution)/shard_map/ppermute | solution.py:378
  31.1 1.0 copy-start.5
  43.5 8.7 %copy-start.3 = (f32[344,336]{1,0:T(8,128)S(1)}, f32[344,336]{1,0:T(8,128)}, u32[]{:S(2)}) copy-start(f32[344,336]{1,0:T(8,128)} %get-tuple-element.21) | copy-start | bytes 1387012
  45.6 17.4 %collective-permute-start.12 = (f32[344,336]{0,1:T(8,128)}, f32[344,336]{0,1:T(8,128)}, u32[]{:S(2)}, u32[]{:S(2)}) collective-permute-start(f32[344,336]{0,1:T(8,128)} %copy.35), channel_id=1, source_target_pairs={{0,1},{3,2},{4,5},{7,6},{8,9},{11,10},{12,13},{15,14},{16,17},{19,... | collective-permute-start | bytes 1387016 | tf_op jit(solution)/shard_map/ppermute | solution.py:378
  49.8 5.4 %copy-start.1 = (f32[344,336]{1,0:T(8,128)S(1)}, f32[344,336]{1,0:T(8,128)}, u32[]{:S(2)}) copy-start(f32[344,336]{1,0:T(8,128)} %get-tuple-element.19) | copy-start | bytes 1387012
  49.8 23.3 %collective-permute-start.4 = (f32[344,336]{0,1:T(8,128)}, f32[344,336]{0,1:T(8,128)}, u32[]{:S(2)}, u32[]{:S(2)}) collective-permute-start(f32[344,336]{0,1:T(8,128)} %copy.19), channel_id=1, source_target_pairs={{0,1},{3,2},{4,5},{7,6},{8,9},{11,10},{12,13},{15,14},{16,17},{19,... | collective-permute-start | bytes 1387016 | tf_op jit(solution)/shard_map/ppermute | solution.py:378
  53.3 10.9 %copy-start.2 = (f32[344,336]{1,0:T(8,128)S(1)}, f32[344,336]{1,0:T(8,128)}, u32[]{:S(2)}) copy-start(f32[344,336]{1,0:T(8,128)} %get-tuple-element.20) | copy-start | bytes 1387012
  53.3 23.6 %collective-permute-start.16 = (f32[344,336]{0,1:T(8,128)}, f32[344,336]{0,1:T(8,128)}, u32[]{:S(2)}, u32[]{:S(2)}) collective-permute-start(f32[344,336]{0,1:T(8,128)} %copy.43), channel_id=1, source_target_pairs={{1,2},{2,1},{5,6},{6,5},{9,10},{10,9},{13,14},{14,13},{17,18},{18,... | collective-permute-start | bytes 1387016 | tf_op jit(solution)/shard_map/ppermute | solution.py:379
  56.2 18.1 %copy-start = (f32[344,336]{1,0:T(8,128)S(1)}, f32[344,336]{1,0:T(8,128)}, u32[]{:S(2)}) copy-start(f32[344,336]{1,0:T(8,128)} %get-tuple-element.18) | copy-start | bytes 1387012
  56.2 24.3 %collective-permute-start.8 = (f32[344,336]{0,1:T(8,128)}, f32[344,336]{0,1:T(8,128)}, u32[]{:S(2)}, u32[]{:S(2)}) collective-permute-start(f32[344,336]{0,1:T(8,128)} %copy.27), channel_id=1, source_target_pairs={{1,2},{2,1},{5,6},{6,5},{9,10},{10,9},{13,14},{14,13},{17,18},{18,... | collective-permute-start | bytes 1387016 | tf_op jit(solution)/shard_map/ppermute | solution.py:379
  65.4 18.9 %collective-permute-start.13 = (f32[344,336]{0,1:T(8,128)}, f32[344,336]{0,1:T(8,128)}, u32[]{:S(2)}, u32[]{:S(2)}) collective-permute-start(f32[344,336]{0,1:T(8,128)} %copy.37), channel_id=1, source_target_pairs={{1,2},{2,1},{5,6},{6,5},{9,10},{10,9},{13,14},{14,13},{17,18},{18,... | collective-permute-start | bytes 1387016 | tf_op jit(solution)/shard_map/ppermute | solution.py:379
  75.4 12.6 %collective-permute-start.5 = (f32[344,336]{0,1:T(8,128)}, f32[344,336]{0,1:T(8,128)}, u32[]{:S(2)}, u32[]{:S(2)}) collective-permute-start(f32[344,336]{0,1:T(8,128)} %copy.21), channel_id=1, source_target_pairs={{1,2},{2,1},{5,6},{6,5},{9,10},{10,9},{13,14},{14,13},{17,18},{18,... | collective-permute-start | bytes 1387016 | tf_op jit(solution)/shard_map/ppermute | solution.py:379
  79.3 18.7 %collective-permute-start.17 = (f32[344,336]{0,1:T(8,128)}, f32[344,336]{0,1:T(8,128)}, u32[]{:S(2)}, u32[]{:S(2)}) collective-permute-start(f32[344,336]{0,1:T(8,128)} %copy.45), channel_id=1, source_target_pairs={{1,0},{2,3},{5,4},{6,7},{9,8},{10,11},{13,12},{14,15},{17,16},{18,... | collective-permute-start | bytes 1387016 | tf_op jit(solution)/shard_map/ppermute | solution.py:381
  82.9 26.1 %collective-permute-start.9 = (f32[344,336]{0,1:T(8,128)}, f32[344,336]{0,1:T(8,128)}, u32[]{:S(2)}, u32[]{:S(2)}) collective-permute-start(f32[344,336]{0,1:T(8,128)} %copy.29), channel_id=1, source_target_pairs={{1,0},{2,3},{5,4},{6,7},{9,8},{10,11},{13,12},{14,15},{17,16},{18,... | collective-permute-start | bytes 1387016 | tf_op jit(solution)/shard_map/ppermute | solution.py:381
  84.2 47.5 %collective-permute-start.3 = (f32[256,336]{1,0:T(8,128)}, f32[256,336]{1,0:T(8,128)}, u32[]{:S(2)}, u32[]{:S(2)}) collective-permute-start(f32[256,336]{1,0:T(8,128)} %get-tuple-element.17), channel_id=1, source_target_pairs={{0,16},{16,0},{1,17},{17,1},{2,18},{18,2},{3,19},{19,3},{4,20},{20... | collective-permute-start | bytes 1032200 | tf_op jit(solution)/shard_map/ppermute | solution.py:424
  86.6 33.5 %collective-permute-start.14 = (f32[344,336]{0,1:T(8,128)}, f32[344,336]{0,1:T(8,128)}, u32[]{:S(2)}, u32[]{:S(2)}) collective-permute-start(f32[344,336]{0,1:T(8,128)} %copy.39), channel_id=1, source_target_pairs={{1,0},{2,3},{5,4},{6,7},{9,8},{10,11},{13,12},{14,15},{17,16},{18,... | collective-permute-start | bytes 1387016 | tf_op jit(solution)/shard_map/ppermute | solution.py:381
  90.4 38.9 %collective-permute-start.6 = (f32[344,336]{0,1:T(8,128)}, f32[344,336]{0,1:T(8,128)}, u32[]{:S(2)}, u32[]{:S(2)}) collective-permute-start(f32[344,336]{0,1:T(8,128)} %copy.23), channel_id=1, source_target_pairs={{1,0},{2,3},{5,4},{6,7},{9,8},{10,11},{13,12},{14,15},{17,16},{18,... | collective-permute-start | bytes 1387016 | tf_op jit(solution)/shard_map/ppermute | solution.py:381
  100.3 39.5 %collective-permute-start.19 = (f32[344,336]{0,1:T(8,128)}, f32[344,336]{0,1:T(8,128)}, u32[]{:S(2)}, u32[]{:S(2)}) collective-permute-start(f32[344,336]{0,1:T(8,128)} %copy.49), channel_id=1, source_target_pairs={{0,16},{16,0},{1,17},{17,1},{2,18},{18,2},{3,19},{19,3},{4,20},{20... | collective-permute-start | bytes 1387016 | tf_op jit(solution)/shard_map/ppermute | solution.py:426
  111.3 29.7 %collective-permute-start.11 = (f32[344,336]{0,1:T(8,128)}, f32[344,336]{0,1:T(8,128)}, u32[]{:S(2)}, u32[]{:S(2)}) collective-permute-start(f32[344,336]{0,1:T(8,128)} %copy.33), channel_id=1, source_target_pairs={{0,16},{16,0},{1,17},{17,1},{2,18},{18,2},{3,19},{19,3},{4,20},{20... | collective-permute-start | bytes 1387016 | tf_op jit(solution)/shard_map/ppermute | solution.py:426
  122.4 19.9 %collective-permute-start.18 = (f32[344,336]{0,1:T(8,128)}, f32[344,336]{0,1:T(8,128)}, u32[]{:S(2)}, u32[]{:S(2)}) collective-permute-start(f32[344,336]{0,1:T(8,128)} %copy.47), channel_id=1, source_target_pairs={{0,16},{16,0},{1,17},{17,1},{2,18},{18,2},{3,19},{19,3},{4,20},{20... | collective-permute-start | bytes 1387016 | tf_op jit(solution)/shard_map/ppermute | solution.py:426
  131.7 12.7 %collective-permute-start.10 = (f32[344,336]{0,1:T(8,128)}, f32[344,336]{0,1:T(8,128)}, u32[]{:S(2)}, u32[]{:S(2)}) collective-permute-start(f32[344,336]{0,1:T(8,128)} %copy.31), channel_id=1, source_target_pairs={{0,16},{16,0},{1,17},{17,1},{2,18},{18,2},{3,19},{19,3},{4,20},{20... | collective-permute-start | bytes 1387016 | tf_op jit(solution)/shard_map/ppermute | solution.py:426
  131.7 2.7 %collective-permute-start.2 = (f32[256,336]{1,0:T(8,128)}, f32[256,336]{1,0:T(8,128)S(1)}, u32[]{:S(2)}, u32[]{:S(2)}) collective-permute-start(f32[256,336]{1,0:T(8,128)} %get-tuple-element.16), channel_id=1, source_target_pairs={{0,16},{16,0},{1,17},{17,1},{2,18},{18,2},{3,19},{19,3},{4,20},{20... | collective-permute-start | bytes 1032200 | tf_op jit(solution)/shard_map/ppermute | solution.py:424
  134.3 0.7 copy-start.7
